TPU v7x, 128 devices: a whole 4x4x4 slice. The times are simulated.
128 devices in a mesh: sub: 16 (over z_lo, y, core), pole: 8 (over x, z_hi).
Axes of the slice: x: 4, y: 4, z: 4 (z_hi: 2, z_lo: 2; z = z_hi * 2 + z_lo), core: 2. Of those that a mesh axis runs over, the one named last changes fastest.
Arguments:
- state: float32 [12288, 512], P('sub'), may hold values from -6 to 6
- conductivity: float32 [12288], P('sub'), may hold values from 0.2 to 2
- pole_shift: float32 [8, 2], P('pole'), may hold values from 0.2 to 1
- pole_weight: float32 [8, 2], P('pole'), may hold values from -1.5 to 1.5
- order_list: int32 [16, 1024], P('sub'), may hold values from 0 to 1023, as said below
- inverse: bfloat16 [8, 12288, 2048], P('pole', 'sub'), may hold values from -0.1 to 0.4
Outputs:
- final_state: float32 [12288, 512], P(('sub', 'pole'))
Inputs may be any that keep to these rules, and one draw needn't show every extreme that they name: `order_list`: row s holds each of 0 to 1023 exactly once.
All inputs are finite; a program needn't handle non-finite values.
Results may differ from a plain program's by a relative error of at most 0.0052.
Values may be sent and summed in bfloat16 or wider, within the bound.
A program may use at most 64 MiB of HBM per device.

v0:
```python
import jax
import jax.numpy as jnp
from jax import lax
from jax.sharding import PartitionSpec as P

H = 128
STEPS = 2


def with_halo(x, sides, width):
    for axis, dim in sides:
        devices, length = (lax.axis_size(axis), x.shape[dim])
        up = [(i, (i + 1) % devices) for i in range(devices - 1)]
        down = [(j, i) for i, j in up]
        last = lax.slice_in_dim(x, length - width, length, axis=dim)
        initial = lax.slice_in_dim(x, 0, width, axis=dim)
        before = lax.ppermute(last, axis, up)
        after = lax.ppermute(initial, axis, down)
        x = jnp.concatenate([before, x, after], axis=dim)
    return x


def in_blocks(x, dim, devices):
    before, after = (x.shape[:dim], x.shape[dim + 1 :])
    return jnp.moveaxis(x.reshape(*before, devices, -1, *after), dim, 0)


def sent_and_summed(x, axis, dim):
    pieces = in_blocks(x, dim, lax.axis_size(axis))
    arrived = lax.all_to_all(pieces, axis, split_axis=0, concat_axis=0, tiled=True)
    return arrived.sum(axis=0)


def in_order(pieces, dim):
    pieces = jnp.moveaxis(pieces, 0, dim)
    dims = pieces.shape
    return pieces.reshape(*dims[:dim], dims[dim] * dims[dim + 1], *dims[dim + 2 :])


def from_everyone(x, axis):
    devices = lax.axis_size(axis)
    return lax.all_to_all(jnp.broadcast_to(x[None], (devices, *x.shape)), axis, 0, 0, tiled=True)


def gathered_copies(x, axis, dim):
    return in_order(from_everyone(x, axis), dim)


def laplace(padded, rim_width):
    inner_count = padded.shape[0] - 2 * rim_width
    middle = padded[rim_width : rim_width + inner_count]
    return (
        4.0 * middle
        - padded[rim_width - 1 : rim_width - 1 + inner_count]
        - padded[rim_width + 1 : rim_width + 1 + inner_count]
        - padded[:inner_count]
        - padded[2 * rim_width : 2 * rim_width + inner_count]
    )


def shifted(padded, sigma_mid, shift_re, shift_im, rim_width):
    laplace_part = laplace(padded, rim_width)
    inner_count = laplace_part.shape[0]
    middle = padded[rim_width : rim_width + inner_count]
    column_half = middle.shape[1] // 2
    real_part = middle[:, :column_half]
    imag_part = middle[:, column_half:]
    sigma_col = sigma_mid[:, None]
    return laplace_part + jnp.concatenate(
        [
            sigma_col * (shift_re * real_part - shift_im * imag_part),
            sigma_col * (shift_im * real_part + shift_re * imag_part),
        ],
        axis=1,
    )


def correct(residual_ext, ordering, inverse_block):
    permuted = jnp.take(residual_ext, ordering, axis=0)
    column_half = permuted.shape[1] // 2
    real_part = permuted[:, :column_half]
    imag_part = permuted[:, column_half:]
    stacked = jnp.concatenate(
        [
            jnp.concatenate([real_part, imag_part], axis=1),
            jnp.concatenate([-imag_part, real_part], axis=1),
        ],
        axis=0,
    )
    return jnp.dot(inverse_block, stacked, preferred_element_type=jnp.float32)


def shards(state, conductivity, pole_shift, pole_weight, order_list, inverse):
    row_count = conductivity.shape[0]
    column_half = state.shape[1]
    pole_count = lax.axis_size("pole")
    share_rows = row_count // pole_count
    ordering = order_list[0]
    inverse_block = inverse[0]
    shift_re = pole_shift[0, 0]
    shift_im = pole_shift[0, 1]
    weight_re = pole_weight[0, 0]
    weight_im = pole_weight[0, 1]
    pole_start = lax.axis_index("pole") * share_rows
    right_side = conductivity[:, None] * state
    result = state[:share_rows]
    for time_step in range(STEPS):
        rhs_ext = with_halo(right_side, (("sub", 0),), H)
        source_ext = jnp.concatenate([rhs_ext, jnp.zeros_like(rhs_ext)], axis=1)
        iterate = correct(source_ext.astype(jnp.bfloat16), ordering, inverse_block)
        padded = with_halo(iterate, (("sub", 0),), H)
        applied = shifted(padded, conductivity, shift_re, shift_im, H)
        own_rows = (source_ext[H : H + row_count] - applied).astype(jnp.bfloat16)
        residual = with_halo(own_rows, (("sub", 0),), H)
        iterate = iterate + correct(residual, ordering, inverse_block)
        partial_value = 2.0 * (
            weight_re * iterate[:, :column_half] - weight_im * iterate[:, column_half:]
        )
        result = sent_and_summed(partial_value, "pole", 0)
        if time_step + 1 < STEPS:
            sigma_share = lax.dynamic_slice_in_dim(conductivity, pole_start, share_rows, 0)
            right_side = gathered_copies(sigma_share[:, None] * result, "pole", 0)
    return result


def solution(mesh):
    placed = (
        P("sub", None),
        P("sub"),
        P("pole", None),
        P("pole", None),
        P("sub", None),
        P("pole", "sub", None),
    )
    return jax.shard_map(
        shards, mesh=mesh, in_specs=placed, out_specs=P(("sub", "pole"), None), check_vma=False
    )
```

profile of v0, /device:TPU:32, one launch (start us, length us, event | category | flops | bytes accessed | tf_op | source)
XLA Modules:
  0.0 235.8 jit_solution(17245840951920931602)
XLA Ops:
  1.8 3.9 %collective-permute-start.1 = (f32[128,512]{1,0:T(8,128)S(1)}, f32[128,512]{1,0:T(8,128)S(1)}, u32[]{:S(2)}, u32[]{:S(2)}) collective-permute-start(f32[128,512]{1,0:T(8,128)S(1)} %get-tuple-element.29), channel_id=1, source_target_pairs={{8,0},{16,8},{24,16},{32,24},{40,32},{48,40},{56,48},{64,56},{72,6... | collective-permute-start | bytes 786440 | tf_op jit(solution)/shard_map/ppermute | solution.py:18
  9.6 5.9 %collective-permute-done = f32[128,512]{1,0:T(8,128)S(1)} collective-permute-done((f32[128,512]{1,0:T(8,128)S(1)}, f32[128,512]{1,0:T(8,128)S(1)}, u32[]{:S(2)}, u32[]{:S(2)}) %collective-permute-start) | collective-permute-done | bytes 262176 | tf_op jit(solution)/shard_map/ppermute | solution.py:17
  17.8 7.9 %gather_fusion = bf16[1024,1024]{1,0:T(8,128)(2,1)} fusion(bf16[1024,1024]{1,0:T(8,128)(2,1)} %fusion.79, s32[1024]{0:T(1024)S(1)} %fusion.73), kind=kCustom, calls=%fused_computation.clone | custom fusion | bytes 4198400 | tf_op jit(solution)/shard_map/jit(_take)/gather | solution.py:79
  27.7 3.5 %fusion.56 = f32[768,1024]{1,0:T(8,128)S(1)} fusion(bf16[1024,512]{1,0:T(8,128)(2,1)S(1)} %get-tuple-element.21, bf16[1024,512]{1,0:T(8,128)(2,1)S(1)} %get-tuple-element.20, bf16[1024,1024]{1,0:T(8,128)(2,1)S(1)} %broadcast_select_fusion.2, bf16[1,768,2048]{2,1,0:T(8,128)(2,1)S(1)} %copy-done), kind=kOutput, calls=%fused_computation.79 | convolution fusion | flops 3233808384 | bytes 10485760 | tf_op jit(solution)/shard_map/dot_general | solution.py:90
  31.3 2.2 collective-permute-start.3
  33.5 2.4 %collective-permute-start.2 = (f32[128,1024]{1,0:T(8,128)S(1)}, f32[128,1024]{1,0:T(8,128)S(1)}, u32[]{:S(2)}, u32[]{:S(2)}) collective-permute-start(f32[128,1024]{1,0:T(8,128)S(1)} %get-tuple-element.12), channel_id=1, source_target_pairs={{0,8},{8,16},{16,24},{24,32},{32,40},{40,48},{48,56},{56,64},{64,7... | collective-permute-start | bytes 1572872 | tf_op jit(solution)/shard_map/ppermute | solution.py:17
  38.1 2.1 collective-permute-done.3
  40.2 5.9 %collective-permute-done.2 = f32[128,1024]{1,0:T(8,128)S(1)} collective-permute-done((f32[128,1024]{1,0:T(8,128)S(1)}, f32[128,1024]{1,0:T(8,128)S(1)}, u32[]{:S(2)}, u32[]{:S(2)}) %collective-permute-start.2) | collective-permute-done | bytes 524320 | tf_op jit(solution)/shard_map/ppermute | solution.py:17
  46.1 4.5 %fusion.44 = bf16[768,1024]{1,0:T(8,128)(2,1)S(1)} fusion(f32[768,1024]{1,0:T(8,128)S(1)} %fusion.56, f32[128,1024]{1,0:T(8,128)S(1)} %collective-permute-done.3, f32[128,1024]{1,0:T(8,128)S(1)} %collective-permute-done.2, f32[1024,1024]{1,0:T(8,128)S(1)} %fusion.4, f32[768,512]{1,0:T(8,128)S(1)} %get-tuple-element.9, f32[768,512]{1,0:T(8,128)S(1)} %get-tuple-element.8), kind=kLoop, calls=%fused_computation.59 | loop fusion | flops 10223616 | bytes 12058624 | tf_op jit(solution)/shard_map/convert_element_type | solution.py:113
  52.6 2.6 %collective-permute-start.4 = (bf16[128,1024]{1,0:T(8,128)(2,1)S(1)}, bf16[128,1024]{1,0:T(8,128)(2,1)S(1)}, u32[]{:S(2)}, u32[]{:S(2)}) collective-permute-start(bf16[128,1024]{1,0:T(8,128)(2,1)S(1)} %get-tuple-element.26), channel_id=1, source_target_pairs={{0,8},{8,16},{16,24},{24,32},{32,40},{40,48},{48,56},{56,64},{64,7... | collective-permute-start | bytes 786440 | tf_op jit(solution)/shard_map/ppermute | solution.py:17
  56.5 5.9 %collective-permute-done.4 = bf16[128,1024]{1,0:T(8,128)(2,1)S(1)} collective-permute-done((bf16[128,1024]{1,0:T(8,128)(2,1)S(1)}, bf16[128,1024]{1,0:T(8,128)(2,1)S(1)}, u32[]{:S(2)}, u32[]{:S(2)}) %collective-permute-start.4) | collective-permute-done | bytes 262176 | tf_op jit(solution)/shard_map/ppermute | solution.py:17
  64.0 7.9 %gather_fusion.1 = bf16[1024,1024]{1,0:T(8,128)(2,1)} fusion(bf16[1024,1024]{1,0:T(8,128)(2,1)} %pad_maximum_fusion.4, s32[1024]{0:T(1024)S(1)} %fusion.73), kind=kCustom, calls=%fused_computation.1.clone | custom fusion | bytes 4198400 | tf_op jit(solution)/shard_map/jit(_take)/gather | solution.py:79
  75.6 3.4 %bitcast_add_fusion.1 = f32[768,1024]{1,0:T(8,128)S(1)} fusion(f32[768,1024]{1,0:T(8,128)S(1)} %copy-done.6, bf16[1024,512]{1,0:T(8,128)(2,1)S(1)} %get-tuple-element.19, bf16[1024,512]{1,0:T(8,128)(2,1)S(1)} %get-tuple-element.18, bf16[1024,1024]{1,0:T(8,128)(2,1)S(1)} %broadcast_select_fusion.1, bf16[1,768,2048]{2,1,0:T(8,128)(2,1)S(1)} %copy-done), kind=kOutput, calls=%fused_computation.67 | convolution fusion | flops 3234594816 | bytes 13631488 | tf_op jit(solution)/shard_map/dot_general | solution.py:90
  79.0 2.8 %fusion.72 = f32[768,512]{1,0:T(8,128)} fusion(f32[768,1024]{1,0:T(8,128)S(1)} %bitcast_add_fusion.1, f32[]{:T(128)} %bitcast.7, f32[]{:T(128)} %bitcast), kind=kLoop, calls=%fused_computation.86 | loop fusion | flops 1572864 | bytes 4718600 | tf_op jit(solution)/shard_map/mul | solution.py:116
  81.9 7.0 %all-to-all-start = ((f32[8,96,512]{2,1,0:T(8,128)}), f32[8,96,512]{2,1,0:T(8,128)}, u32[]{:S(2)}, u32[]{:S(2)}) async-start(f32[8,96,512]{2,1,0:T(8,128)} %bitcast.36), calls=%async_computation | async-start | bytes 3145728 | tf_op jit(solution)/shard_map/all_to_all | solution.py:30
  88.9 18.7 %all-to-all-done = f32[8,96,512]{2,1,0:T(8,128)} async-done(((f32[8,96,512]{2,1,0:T(8,128)}), f32[8,96,512]{2,1,0:T(8,128)}, u32[]{:S(2)}, u32[]{:S(2)}) %all-to-all-start) | async-done | bytes 1572896 | tf_op jit(solution)/shard_map/all_to_all | solution.py:30
  109.5 24.8 %all_to_all.15 = f32[8,96,512]{2,1,0:T(8,128)S(1)} all-to-all(f32[8,96,512]{2,1,0:T(8,128)S(1)} %broadcast_in_dim.11), channel_id=1, replica_groups=mesh['sub'=16,'pole'=8] {'pole'}, dimensions={0} | all-to-all | bytes 3145728 | tf_op jit(solution)/shard_map/all_to_all | solution.py:42
  134.3 2.2 collective-permute-start.7
  136.6 2.1 collective-permute-start.6
  140.5 5.9 %collective-permute-done.6 = f32[128,512]{1,0:T(8,128)S(1)} collective-permute-done((f32[128,512]{1,0:T(8,128)S(1)}, f32[128,512]{1,0:T(8,128)S(1)}, u32[]{:S(2)}, u32[]{:S(2)}) %collective-permute-start.6) | collective-permute-done | bytes 262176 | tf_op jit(solution)/shard_map/ppermute | solution.py:17
  148.7 7.9 %gather_fusion.2 = bf16[1024,1024]{1,0:T(8,128)(2,1)} fusion(bf16[1024,1024]{1,0:T(8,128)(2,1)} %fusion.78, s32[1024]{0:T(1024)S(1)} %fusion.73), kind=kCustom, calls=%fused_computation.2.clone | custom fusion | bytes 4198400 | tf_op jit(solution)/shard_map/jit(_take)/gather | solution.py:79
  158.6 3.5 %fusion.51 = f32[768,1024]{1,0:T(8,128)S(1)} fusion(bf16[1024,512]{1,0:T(8,128)(2,1)S(1)} %get-tuple-element.17, bf16[1024,512]{1,0:T(8,128)(2,1)S(1)} %get-tuple-element.16, bf16[1024,1024]{1,0:T(8,128)(2,1)S(1)} %broadcast_select_fusion.3, bf16[1,768,2048]{2,1,0:T(8,128)(2,1)S(1)} %copy-done), kind=kOutput, calls=%fused_computation.78 | convolution fusion | flops 3233808384 | bytes 10485760 | tf_op jit(solution)/shard_map/dot_general | solution.py:90
  162.2 2.2 collective-permute-start.9
  164.4 2.6 %collective-permute-start.8 = (f32[128,1024]{1,0:T(8,128)S(1)}, f32[128,1024]{1,0:T(8,128)S(1)}, u32[]{:S(2)}, u32[]{:S(2)}) collective-permute-start(f32[128,1024]{1,0:T(8,128)S(1)} %get-tuple-element.10), channel_id=1, source_target_pairs={{0,8},{8,16},{16,24},{24,32},{32,40},{40,48},{48,56},{56,64},{64,7... | collective-permute-start | bytes 1572872 | tf_op jit(solution)/shard_map/ppermute | solution.py:17
  171.1 5.9 %collective-permute-done.8 = f32[128,1024]{1,0:T(8,128)S(1)} collective-permute-done((f32[128,1024]{1,0:T(8,128)S(1)}, f32[128,1024]{1,0:T(8,128)S(1)}, u32[]{:S(2)}, u32[]{:S(2)}) %collective-permute-start.8) | collective-permute-done | bytes 524320 | tf_op jit(solution)/shard_map/ppermute | solution.py:17
  177.0 4.5 %fusion.35 = bf16[768,1024]{1,0:T(8,128)(2,1)S(1)} fusion(f32[768,1024]{1,0:T(8,128)S(1)} %fusion.51, f32[128,1024]{1,0:T(8,128)S(1)} %collective-permute-done.9, f32[128,1024]{1,0:T(8,128)S(1)} %collective-permute-done.8, f32[1024,1024]{1,0:T(8,128)S(1)} %select_maximum_fusion, f32[768,512]{1,0:T(8,128)S(1)} %get-tuple-element.7, ...), kind=kLoop, calls=%fused_computation.50 | loop fusion | flops 10223616 | bytes 12058624 | tf_op jit(solution)/shard_map/convert_element_type | solution.py:113
  183.5 2.4 %collective-permute-start.10 = (bf16[128,1024]{1,0:T(8,128)(2,1)S(1)}, bf16[128,1024]{1,0:T(8,128)(2,1)S(1)}, u32[]{:S(2)}, u32[]{:S(2)}) collective-permute-start(bf16[128,1024]{1,0:T(8,128)(2,1)S(1)} %get-tuple-element.22), channel_id=1, source_target_pairs={{0,8},{8,16},{16,24},{24,32},{32,40},{40,48},{48,56},{56,64},{64,7... | collective-permute-start | bytes 786440 | tf_op jit(solution)/shard_map/ppermute | solution.py:17
  187.4 5.9 %collective-permute-done.10 = bf16[128,1024]{1,0:T(8,128)(2,1)S(1)} collective-permute-done((bf16[128,1024]{1,0:T(8,128)(2,1)S(1)}, bf16[128,1024]{1,0:T(8,128)(2,1)S(1)}, u32[]{:S(2)}, u32[]{:S(2)}) %collective-permute-start.10) | collective-permute-done | bytes 262176 | tf_op jit(solution)/shard_map/ppermute | solution.py:17
  194.8 7.9 %gather_fusion.3 = bf16[1024,1024]{1,0:T(8,128)(2,1)} fusion(bf16[1024,1024]{1,0:T(8,128)(2,1)} %pad_maximum_fusion.5, s32[1024]{0:T(1024)S(1)} %fusion.73), kind=kCustom, calls=%fused_computation.3.clone | custom fusion | bytes 4198400 | tf_op jit(solution)/shard_map/jit(_take)/gather | solution.py:79
  206.4 3.4 %bitcast_add_fusion = f32[768,1024]{1,0:T(8,128)S(1)} fusion(f32[768,1024]{1,0:T(8,128)S(1)} %copy-done.8, bf16[1024,512]{1,0:T(8,128)(2,1)S(1)} %get-tuple-element.15, bf16[1024,512]{1,0:T(8,128)(2,1)S(1)} %get-tuple-element.14, bf16[1024,1024]{1,0:T(8,128)(2,1)S(1)} %broadcast_select_fusion, bf16[1,768,2048]{2,1,0:T(8,128)(2,1)S(1)} %copy-done), kind=kOutput, calls=%fused_computation.66 | convolution fusion | flops 3234594816 | bytes 13631488 | tf_op jit(solution)/shard_map/dot_general | solution.py:90
  211.6 22.0 %all_to_all.16 = f32[8,96,512]{2,1,0:T(8,128)} all-to-all(f32[8,96,512]{2,1,0:T(8,128)S(1)} %bitcast.37), channel_id=1, replica_groups=mesh['sub'=16,'pole'=8] {'pole'}, dimensions={0} | all-to-all | bytes 3145728 | tf_op jit(solution)/shard_map/all_to_all | solution.py:30
  233.5 2.2 reduce_sum.19
  (74 shorter events, 43.2 us)
Async XLA Ops:
  0.0 27.7 %copy-start = (bf16[1,768,2048]{2,1,0:T(8,128)(2,1)S(1)}, bf16[1,768,2048]{2,1,0:T(8,128)(2,1)}, u32[]{:S(2)}) copy-start(bf16[1,768,2048]{2,1,0:T(8,128)(2,1)} %param.13) | copy-start | bytes 9437188
  0.0 7.6 %copy-start.14 = (s32[1,1024]{1,0:T(1,128)S(1)}, s32[1,1024]{1,0:T(1,128)}, u32[]{:S(2)}) copy-start(s32[1,1024]{1,0:T(1,128)} %param.12) | copy-start | bytes 12292
  0.0 7.7 %copy-start.15 = (f32[1,2]{1,0:T(1,128)S(1)}, f32[1,2]{1,0:T(1,128)}, u32[]{:S(2)}) copy-start(f32[1,2]{1,0:T(1,128)} %param.10) | copy-start | bytes 28
  1.7 13.8 %copy-start.1 = (f32[768,512]{1,0:T(8,128)}, f32[768,512]{1,0:T(8,128)S(1)}, u32[]{:S(2)}) copy-start(f32[768,512]{1,0:T(8,128)S(1)} %broadcast_multiply_fusion) | copy-start | bytes 4718596
  1.8 7.8 %collective-permute-start.1 = (f32[128,512]{1,0:T(8,128)S(1)}, f32[128,512]{1,0:T(8,128)S(1)}, u32[]{:S(2)}, u32[]{:S(2)}) collective-permute-start(f32[128,512]{1,0:T(8,128)S(1)} %get-tuple-element.29), channel_id=1, source_target_pairs={{8,0},{16,8},{24,16},{32,24},{40,32},{48,40},{56,48},{64,56},{72,6... | collective-permute-start | bytes 786440 | tf_op jit(solution)/shard_map/ppermute | solution.py:18
  5.7 9.8 %collective-permute-start = (f32[128,512]{1,0:T(8,128)S(1)}, f32[128,512]{1,0:T(8,128)S(1)}, u32[]{:S(2)}, u32[]{:S(2)}) collective-permute-start(f32[128,512]{1,0:T(8,128)S(1)} %get-tuple-element.28), channel_id=1, source_target_pairs={{0,8},{8,16},{16,24},{24,32},{32,40},{40,48},{48,56},{56,64},{64,7... | collective-permute-start | bytes 786440 | tf_op jit(solution)/shard_map/ppermute | solution.py:17
  15.5 0.7 copy-start.9
  27.7 8.2 %copy-start.10 = (f32[128,512]{1,0:T(8,128)S(1)}, f32[128,512]{1,0:T(8,128)}, u32[]{:S(2)}) copy-start(f32[128,512]{1,0:T(8,128)} %copy-done.9) | copy-start | bytes 786436
  31.2 14.9 %copy-start.5 = (f32[768,1024]{1,0:T(8,128)}, f32[768,1024]{1,0:T(8,128)S(1)}, u32[]{:S(2)}) copy-start(f32[768,1024]{1,0:T(8,128)S(1)} %fusion.56) | copy-start | bytes 9437188
  31.2 4.8 %copy-start.2 = (f32[768,512]{1,0:T(8,128)S(1)}, f32[768,512]{1,0:T(8,128)}, u32[]{:S(2)}) copy-start(f32[768,512]{1,0:T(8,128)} %copy-done.1) | copy-start | bytes 4718596
  31.3 8.9 %collective-permute-start.3 = (f32[128,1024]{1,0:T(8,128)S(1)}, f32[128,1024]{1,0:T(8,128)S(1)}, u32[]{:S(2)}, u32[]{:S(2)}) collective-permute-start(f32[128,1024]{1,0:T(8,128)S(1)} %get-tuple-element.13), channel_id=1, source_target_pairs={{8,0},{16,8},{24,16},{32,24},{40,32},{48,40},{56,48},{64,56},{72,6... | collective-permute-start | bytes 1572872 | tf_op jit(solution)/shard_map/ppermute | solution.py:18
  33.5 3.0 %copy-start.13 = (f32[768]{0:T(1024)S(1)}, f32[768]{0:T(1024)}, u32[]{:S(2)}) copy-start(f32[768]{0:T(1024)} %param.9) | copy-start | bytes 9220
  33.5 12.6 %collective-permute-start.2 = (f32[128,1024]{1,0:T(8,128)S(1)}, f32[128,1024]{1,0:T(8,128)S(1)}, u32[]{:S(2)}, u32[]{:S(2)}) collective-permute-start(f32[128,1024]{1,0:T(8,128)S(1)} %get-tuple-element.12), channel_id=1, source_target_pairs={{0,8},{8,16},{16,24},{24,32},{32,40},{40,48},{48,56},{56,64},{64,7... | collective-permute-start | bytes 1572872 | tf_op jit(solution)/shard_map/ppermute | solution.py:17
  46.1 9.1 %copy-start.16 = (f32[1,2]{1,0:T(1,128)S(1)}, f32[1,2]{1,0:T(1,128)}, u32[]{:S(2)}) copy-start(f32[1,2]{1,0:T(1,128)} %param.11) | copy-start | bytes 28
  50.7 5.8 %collective-permute-start.5 = (bf16[128,1024]{1,0:T(8,128)(2,1)S(1)}, bf16[128,1024]{1,0:T(8,128)(2,1)S(1)}, u32[]{:S(2)}, u32[]{:S(2)}) collective-permute-start(bf16[128,1024]{1,0:T(8,128)(2,1)S(1)} %get-tuple-element.27), channel_id=1, source_target_pairs={{8,0},{16,8},{24,16},{32,24},{40,32},{48,40},{56,48},{64,56},{72,6... | collective-permute-start | bytes 786440 | tf_op jit(solution)/shard_map/ppermute | solution.py:18
  52.6 9.8 %collective-permute-start.4 = (bf16[128,1024]{1,0:T(8,128)(2,1)S(1)}, bf16[128,1024]{1,0:T(8,128)(2,1)S(1)}, u32[]{:S(2)}, u32[]{:S(2)}) collective-permute-start(bf16[128,1024]{1,0:T(8,128)(2,1)S(1)} %get-tuple-element.26), channel_id=1, source_target_pairs={{0,8},{8,16},{16,24},{24,32},{32,40},{40,48},{48,56},{56,64},{64,7... | collective-permute-start | bytes 786440 | tf_op jit(solution)/shard_map/ppermute | solution.py:17
  73.7 1.9 copy-start.6
  81.9 25.8 %all-to-all-start = ((f32[8,96,512]{2,1,0:T(8,128)}), f32[8,96,512]{2,1,0:T(8,128)}, u32[]{:S(2)}, u32[]{:S(2)}) async-start(f32[8,96,512]{2,1,0:T(8,128)} %bitcast.36), calls=%async_computation | async-start | bytes 3145728 | tf_op jit(solution)/shard_map/all_to_all | solution.py:30
  134.3 12.1 %copy-start.3 = (f32[8,96,512]{2,1,0:T(8,128)}, f32[8,96,512]{2,1,0:T(8,128)S(1)}, u32[]{:S(2)}) copy-start(f32[8,96,512]{2,1,0:T(8,128)S(1)} %all_to_all.15) | copy-start | bytes 4718596
  134.3 6.1 %collective-permute-start.7 = (f32[128,512]{1,0:T(8,128)S(1)}, f32[128,512]{1,0:T(8,128)S(1)}, u32[]{:S(2)}, u32[]{:S(2)}) collective-permute-start(f32[128,512]{1,0:T(8,128)S(1)} %get-tuple-element.25), channel_id=1, source_target_pairs={{8,0},{16,8},{24,16},{32,24},{40,32},{48,40},{56,48},{64,56},{72,6... | collective-permute-start | bytes 786440 | tf_op jit(solution)/shard_map/ppermute | solution.py:18
  136.6 9.8 %collective-permute-start.6 = (f32[128,512]{1,0:T(8,128)S(1)}, f32[128,512]{1,0:T(8,128)S(1)}, u32[]{:S(2)}, u32[]{:S(2)}) collective-permute-start(f32[128,512]{1,0:T(8,128)S(1)} %get-tuple-element.24), channel_id=1, source_target_pairs={{0,8},{8,16},{16,24},{24,32},{32,40},{40,48},{48,56},{56,64},{64,7... | collective-permute-start | bytes 786440 | tf_op jit(solution)/shard_map/ppermute | solution.py:17
  146.4 0.7 copy-start.11
  158.6 8.4 %copy-start.12 = (f32[128,512]{1,0:T(8,128)S(1)}, f32[128,512]{1,0:T(8,128)}, u32[]{:S(2)}) copy-start(f32[128,512]{1,0:T(8,128)} %copy-done.11) | copy-start | bytes 786436
  162.1 14.9 %copy-start.7 = (f32[768,1024]{1,0:T(8,128)}, f32[768,1024]{1,0:T(8,128)S(1)}, u32[]{:S(2)}) copy-start(f32[768,1024]{1,0:T(8,128)S(1)} %fusion.51) | copy-start | bytes 9437188
  162.1 5.0 %copy-start.4 = (f32[8,96,512]{2,1,0:T(8,128)S(1)}, f32[8,96,512]{2,1,0:T(8,128)}, u32[]{:S(2)}) copy-start(f32[8,96,512]{2,1,0:T(8,128)} %copy-done.3) | copy-start | bytes 4718596
  162.2 8.9 %collective-permute-start.9 = (f32[128,1024]{1,0:T(8,128)S(1)}, f32[128,1024]{1,0:T(8,128)S(1)}, u32[]{:S(2)}, u32[]{:S(2)}) collective-permute-start(f32[128,1024]{1,0:T(8,128)S(1)} %get-tuple-element.11), channel_id=1, source_target_pairs={{8,0},{16,8},{24,16},{32,24},{40,32},{48,40},{56,48},{64,56},{72,6... | collective-permute-start | bytes 1572872 | tf_op jit(solution)/shard_map/ppermute | solution.py:18
  164.4 12.6 %collective-permute-start.8 = (f32[128,1024]{1,0:T(8,128)S(1)}, f32[128,1024]{1,0:T(8,128)S(1)}, u32[]{:S(2)}, u32[]{:S(2)}) collective-permute-start(f32[128,1024]{1,0:T(8,128)S(1)} %get-tuple-element.10), channel_id=1, source_target_pairs={{0,8},{8,16},{16,24},{24,32},{32,40},{40,48},{48,56},{56,64},{64,7... | collective-permute-start | bytes 1572872 | tf_op jit(solution)/shard_map/ppermute | solution.py:17
  181.6 5.8 %collective-permute-start.11 = (bf16[128,1024]{1,0:T(8,128)(2,1)S(1)}, bf16[128,1024]{1,0:T(8,128)(2,1)S(1)}, u32[]{:S(2)}, u32[]{:S(2)}) collective-permute-start(bf16[128,1024]{1,0:T(8,128)(2,1)S(1)} %get-tuple-element.23), channel_id=1, source_target_pairs={{8,0},{16,8},{24,16},{32,24},{40,32},{48,40},{56,48},{64,56},{72,6... | collective-permute-start | bytes 786440 | tf_op jit(solution)/shard_map/ppermute | solution.py:18
  183.5 9.8 %collective-permute-start.10 = (bf16[128,1024]{1,0:T(8,128)(2,1)S(1)}, bf16[128,1024]{1,0:T(8,128)(2,1)S(1)}, u32[]{:S(2)}, u32[]{:S(2)}) collective-permute-start(bf16[128,1024]{1,0:T(8,128)(2,1)S(1)} %get-tuple-element.22), channel_id=1, source_target_pairs={{0,8},{8,16},{16,24},{24,32},{32,40},{40,48},{48,56},{56,64},{64,7... | collective-permute-start | bytes 786440 | tf_op jit(solution)/shard_map/ppermute | solution.py:17
  204.5 1.9 copy-start.8
where the time goes:
time: 237 us; the launch traced here: 236 us
  waiting for transfers between devices  63.5 us (27%)
  blocking collectives  46.8 us (20%)
  local copies, waits for them, and re-layouts  38.1 us (16%)
  other arithmetic  37.7 us (16%)
  starting transfers between devices  35.4 us (15%)
  matrix products  13.8 us (6%)
    ppermute x6, waiting for transfers between devices, with_halo(): before = lax.ppermute(last, axis, up)  35.6 us
    gather x4, local copies, waits for them, and re-layouts, correct(): permuted = jnp.take(residual_ext, ordering, axis=0)  31.4 us
    all_to_all x1, blocking collectives, from_everyone(): lax.all_to_all(jnp.broadcast_to(x[None], (devices, *x.shape)), axis, 0, 0...  24.8 us
    all_to_all x1, blocking collectives, sent_and_summed(): lax.all_to_all(pieces, axis, split_axis=0, concat_axis=0, tiled=True)  22 us
    all_to_all x1, waiting for transfers between devices, sent_and_summed(): lax.all_to_all(pieces, axis, split_axis=0, concat_axis=0, tiled=True)  18.7 us
    ppermute x6, starting transfers between devices, with_halo(): after = lax.ppermute(initial, axis, down)  14.4 us
    ppermute x6, starting transfers between devices, with_halo(): before = lax.ppermute(last, axis, up)  14 us
    dot_general x4, matrix products, correct(): return jnp.dot(inverse_block, stacked, preferred_element_type=jnp.float32)  13.8 us
  transfers between devices with their start and end apart: 13, of which 13 were waited for; matrix products, arithmetic and copies ran while one was open for 2% of the time, Pallas kernels for 0%

commit v1 on v0

v1 whole, which is shorter than its diff:
```python
import jax
import jax.numpy as jnp
from jax import lax
from jax.experimental import pallas as pl
from jax.experimental.pallas import tpu as pltpu
from jax.sharding import PartitionSpec as P

MESH = pl.DeviceIdType.MESH
F32 = jnp.float32
BF16 = jnp.bfloat16
H = 128
N = 128
PEERS = ((2, 1), (1, 1), (3, 1), (2, 0), (0, 1), (1, 0), (3, 0))
EVERY = PEERS + ((0, 0),)
I16 = jnp.int16
TOP = 32767.0


def rounded(x):
    return x.astype(BF16)


def coded(v, peak):
    return jnp.round(v * (TOP / peak)).astype(jnp.int32).astype(I16)


def peak_of(v):
    return jnp.maximum(jnp.max(jnp.abs(v), axis=0, keepdims=True), 1e-30)


def decoded(q, peak):
    return q.astype(jnp.int32).astype(F32) * (peak * (1.0 / TOP))


def kernel(
    chunks, order_ref, cond_ref, shift_ref, weight_ref, state_hbm, inv_hbm, out_ref,
    g_in, st, cb, gp, e1, hs, x, acc, rp, p1s, p1r, p1sp, p1rp, e2, rss, rsr, rssp, rsrp,
    ags, agr, agsp, agrp, nbs,
    in_sem, halo_ss, halo_rs, p1_ss, p1_rs, rs_ss, rs_rs, ag_ss, ag_rs, nb_ss, nb_rs,
):
    s = lax.axis_index("sub")
    p = lax.axis_index("pole")
    px, pz = p // 2, lax.rem(p, 2)
    subs = lax.axis_size("sub")
    has_up, has_down = s > 0, s < subs - 1
    up, down = lax.rem(s + subs - 1, subs), lax.rem(s + 1, subs)

    def pole_at(dx, dz):
        return lax.rem(px + dx, 4) * 2 + lax.rem(pz + dz, 2)

    def remote(src, dst, send_sem, recv_sem, sub, pole):
        return pltpu.make_async_remote_copy(
            src_ref=src, dst_ref=dst, send_sem=send_sem, recv_sem=recv_sem,
            device_id=(sub, pole), device_id_type=MESH,
        )

    state_in = [
        pltpu.make_async_copy(state_hbm.at[:, pl.ds(c * N, N)], st.at[c], in_sem.at[c])
        for c in range(chunks)
    ]
    for copy in state_in:
        copy.start()
    g_copy = pltpu.make_async_copy(inv_hbm.at[0], g_in, in_sem.at[chunks])
    g_copy.start()

    barrier = pltpu.get_barrier_semaphore()
    for dx, dz in EVERY:
        q = pole_at(dx, dz)
        if (dx, dz) != (0, 0):
            pl.semaphore_signal(barrier, inc=1, device_id=(s, q), device_id_type=MESH)
        pl.semaphore_signal(barrier, inc=1, device_id=(up, q), device_id_type=MESH)
        pl.semaphore_signal(barrier, inc=1, device_id=(down, q), device_id_type=MESH)

    shift_re, shift_im = shift_ref[0, 0], shift_ref[0, 1]
    w_re, w_im = 2.0 * weight_ref[0, 0], 2.0 * weight_ref[0, 1]

    for b in range(6):
        row = cond_ref[:, 128 * b : 128 * b + 128]
        cb[128 * b : 128 * b + 128, :] = jnp.broadcast_to(row, (128, 128)).T

    for c in range(chunks):
        for d in range(2):
            x[c, d, 0:8, :] = jnp.zeros((8, N), F32)
            x[c, d, 776:784, :] = jnp.zeros((8, N), F32)

    @pl.when(jnp.logical_not(has_up))
    def _():
        for t in range(2):
            for c in range(chunks):
                e1[t, c, 768:896, :] = jnp.zeros((H, N), BF16)
                p1r[t, c, 0] = jnp.zeros((4, H, N), I16)
                p1rp[t, c, 0] = jnp.zeros((4, N), F32)

    @pl.when(jnp.logical_not(has_down))
    def _():
        for t in range(2):
            for c in range(chunks):
                e1[t, c, 896:1024, :] = jnp.zeros((H, N), BF16)
                p1r[t, c, 1] = jnp.zeros((4, H, N), I16)
                p1rp[t, c, 1] = jnp.zeros((4, N), F32)

    for copy in state_in:
        copy.wait()

    def first_source(c, _):
        src = cb[...] * st[c]
        st[c] = src
        e1[0, c, 0:512, :] = rounded(src[128:640])
        top = rounded(src[0:128])
        bottom = rounded(src[640:768])
        hs[c, 0] = top
        hs[c, 1] = bottom
        for q in range(8):
            e1[0, c, 512 + 32 * q : 528 + 32 * q, :] = top[16 * q : 16 * q + 16]
            e1[0, c, 528 + 32 * q : 544 + 32 * q, :] = bottom[16 * q : 16 * q + 16]
        return 0

    lax.fori_loop(0, chunks, first_source, 0)
    pl.semaphore_wait(barrier, 23)

    def halo_copy(c, d):
        return remote(
            hs.at[c, d], e1.at[0, c, pl.ds(896 - 128 * d, H)], halo_ss.at[c, d], halo_rs.at[c, d],
            down if d else up, p,
        )

    class Several:
        def __init__(self, *copies):
            self.copies = copies

        def start(self):
            for copy in self.copies:
                copy.start()

        def wait_recv(self):
            for copy in self.copies:
                copy.wait_recv()

        def wait_send(self):
            for copy in self.copies:
                copy.wait_send()

    def edge_copy(t, c, d):
        to = down if d else up
        return Several(
            remote(p1sp.at[t, c, d], p1rp.at[t, c, 1 - d], p1_ss.at[t, c, d, 1], p1_rs.at[t, c, d, 1], to, p),
            remote(p1s.at[t, c, d], p1r.at[t, c, 1 - d], p1_ss.at[t, c, d, 0], p1_rs.at[t, c, d, 0], to, p),
        )

    def start_both(make, *args):
        @pl.when(has_up)
        def _():
            make(*args, 0).start()

        @pl.when(has_down)
        def _():
            make(*args, 1).start()

    def wait_recv_both(make, *args):
        @pl.when(has_up)
        def _():
            make(*args, 1).wait_recv()

        @pl.when(has_down)
        def _():
            make(*args, 0).wait_recv()

    def wait_send_both(make, *args):
        @pl.when(has_up)
        def _():
            make(*args, 0).wait_send()

        @pl.when(has_down)
        def _():
            make(*args, 1).wait_send()

    def start_halo(c, _):
        start_both(halo_copy, c)
        return 0

    lax.fori_loop(0, chunks, start_halo, 0)

    g_copy.wait()

    def extended_row(base, count):
        return lax.broadcasted_iota(jnp.int32, (count, 1), 0) + base

    for blk in range(4):
        if blk < 2:
            rows = extended_row(256 + 256 * blk, 256)
        elif blk == 2:
            rows = jnp.concatenate(
                [extended_row(b + 16 * q, 16) for q in range(8) for b in (128, 768)], axis=0
            )
        else:
            rows = jnp.concatenate([extended_row(0, 128), extended_row(896, 128)], axis=0)
        hot = jnp.where(rows == order_ref[...], 1.0, 0.0).astype(BF16)
        at = 256 * blk
        for m in range(2):
            r0 = 384 * m
            re = lax.dot_general(
                g_in[r0 : r0 + 384, 0:1024], hot, (((1,), (1,)), ((), ())), preferred_element_type=F32
            )
            im = lax.dot_general(
                g_in[r0 : r0 + 384, 1024:2048], hot, (((1,), (1,)), ((), ())), preferred_element_type=F32
            )
            gp[r0 : r0 + 384, at : at + 256] = rounded(re)
            gp[768 + r0 : 768 + r0 + 384, at : at + 256] = rounded(im)

    def sweep_one(t, c):
        y = jnp.dot(gp[...], e1[t, c], preferred_element_type=F32)
        x[c, 0, 8:776, :] = y[:768]
        x[c, 1, 8:776, :] = y[768:]

    def residual(t, c):
        for b in (0, 5, 1, 2, 3, 4):
            at = 8 + 128 * b

            def lap(d):
                v = (
                    4.0 * x[c, d, at : at + 128, :]
                    - x[c, d, at - 1 : at + 127, :]
                    - x[c, d, at + 1 : at + 129, :]
                )
                if b > 0:
                    v = v - x[c, d, at - 128 : at, :]
                if b < 5:
                    v = v - x[c, d, at + 128 : at + 256, :]
                return v

            xr = x[c, 0, at : at + 128, :]
            xi = x[c, 1, at : at + 128, :]
            sigma = cb[128 * b : 128 * b + 128, :]
            src = st[c, 128 * b : 128 * b + 128, :]
            rr = src - lap(0) - sigma * (shift_re * xr - shift_im * xi)
            ri = -lap(1) - sigma * (shift_im * xr + shift_re * xi)
            acc[c, 128 * b : 128 * b + 128, :] = w_re * xr - w_im * xi
            if 0 < b < 5:
                e2[c, 128 * (b - 1) : 128 * b, 0:N] = rounded(rr)
                e2[c, 128 * (b - 1) : 128 * b, N : 2 * N] = rounded(ri)
            else:
                d = 0 if b == 0 else 1
                rp[c, d, 0] = rr
                rp[c, d, 1] = ri
                for i, v in enumerate((xr, xi, rr, ri)):
                    peak = peak_of(v)
                    p1sp[t, c, d, i : i + 1, :] = peak
                    p1s[t, c, d, i] = coded(v, peak)
        start_both(edge_copy, t, c)

    def weighted(y):
        re = y[:768, 0:N] - y[768:, N : 2 * N]
        im = y[:768, N : 2 * N] + y[768:, 0:N]
        return w_re * re - w_im * im

    def inner_product(c, _):
        acc[c] += weighted(jnp.dot(gp[:, 0:512], e2[c, 0:512, :], preferred_element_type=F32))
        return 0

    row_of = lax.broadcasted_iota(jnp.int32, (H, 1), 0)
    up_on = jnp.where(has_up, 1.0, 0.0).astype(F32)
    down_on = jnp.where(has_down, 1.0, 0.0).astype(F32)

    def rs_copy(t, c, k):
        q = pole_at(*PEERS[k])
        return Several(
            remote(rssp.at[t, c], rsrp.at[t, c, k], rs_ss.at[t, c, k, 1], rs_rs.at[t, c, k, 1], s, q),
            remote(rss.at[t, c, q], rsr.at[t, c, k], rs_ss.at[t, c, k, 0], rs_rs.at[t, c, k, 0], s, q),
        )

    def finish(t, c):
        wait_recv_both(edge_copy, t, c)
        for d in range(2):
            base = 512
            to = slice(N * d, N * d + N)

            def came(side, i):
                return decoded(p1r[t, c, side, i], p1rp[t, c, side, i : i + 1, :])

            above, below = came(0, d), came(1, d)
            top = rp[c, 0, d] + above + jnp.where(row_of == 0, above[127:128], 0.0)
            bottom = rp[c, 1, d] + below + jnp.where(row_of == 127, below[0:1], 0.0)
            top, bottom = rounded(top), rounded(bottom)
            for q in range(8):
                e2[c, base + 32 * q : base + 32 * q + 16, to] = top[16 * q : 16 * q + 16]
                e2[c, base + 32 * q + 16 : base + 32 * q + 32, to] = bottom[16 * q : 16 * q + 16]
            first = x[c, d, 8:136, :]
            final = x[c, d, 648:776, :]
            over = came(0, 2 + d) + first + jnp.where(row_of == 127, first[0:1], 0.0)
            under = came(1, 2 + d) + final + jnp.where(row_of == 0, final[127:128], 0.0)
            e2[c, base + 256 : base + 384, to] = rounded(up_on * over)
            e2[c, base + 384 : base + 512, to] = rounded(down_on * under)
        total = acc[c] + weighted(jnp.dot(gp[:, 512:1024], e2[c, 512:1024, :], preferred_element_type=F32))
        peak = peak_of(total)
        rssp[t, c] = peak
        total = coded(total, peak)
        for q in range(8):
            if t == 0:
                rss[t, c, q, 0:64, :] = total[128 + 64 * q : 192 + 64 * q]
                rss[t, c, q, 64:80, :] = total[16 * q : 16 * q + 16]
                rss[t, c, q, 80:96, :] = total[640 + 16 * q : 656 + 16 * q]
            else:
                rss[t, c, q] = total[96 * q : 96 * q + 96]
        for k in range(7):
            rs_copy(t, c, k).start()

    def summed(t, c):
        total = decoded(rss[t, c, p], rssp[t, c])
        for k in range(7):
            rs_copy(t, c, k).wait_recv()
        for k in range(7):
            total = total + decoded(rsr[t, c, k], rsrp[t, c, k])
        return total

    def ag_copy(c, k):
        q = pole_at(*PEERS[k])
        return Several(
            remote(agsp.at[c], agrp.at[c, k], ag_ss.at[c, k, 1], ag_rs.at[c, k, 1], s, q),
            remote(ags.at[c], agr.at[c, k], ag_ss.at[c, k, 0], ag_rs.at[c, k, 0], s, q),
        )

    def margin_copy(c, k, d):
        q = pole_at(*EVERY[k])
        src = nbs.at[c, d]
        dst = e1.at[1, c, pl.ds(pl.multiple_of(896 - 128 * d + 16 * p, 16), 16)]
        return remote(src, dst, nb_ss.at[c, k, d], nb_rs.at[c, k, d], down if d else up, q)

    def placed_share(c, q, share):
        st[c, pl.ds(pl.multiple_of(128 + 64 * q, 64), 64), :] = share[0:64]
        st[c, pl.ds(pl.multiple_of(16 * q, 16), 16), :] = share[64:80]
        st[c, pl.ds(pl.multiple_of(640 + 16 * q, 16), 16), :] = share[80:96]
        share = rounded(share)
        e1[1, c, pl.ds(pl.multiple_of(64 * q, 64), 64), :] = share[0:64]
        e1[1, c, pl.ds(pl.multiple_of(512 + 32 * q, 32), 32), :] = share[64:96]

    def next_source(c, _):
        total = summed(0, c)
        sigma = jnp.concatenate(
            [
                cb[pl.ds(pl.multiple_of(128 + 64 * p, 64), 64), :],
                cb[pl.ds(pl.multiple_of(16 * p, 16), 16), :],
                cb[pl.ds(pl.multiple_of(640 + 16 * p, 16), 16), :],
            ],
            axis=0,
        )
        share = sigma * total
        peak = peak_of(share)
        agsp[c] = peak
        ags[c] = coded(share, peak)
        edges = rounded(share[64:96])
        nbs[c, 0] = edges[0:16]
        nbs[c, 1] = edges[16:32]
        for k in range(7):
            ag_copy(c, k).start()

        @pl.when(has_up)
        def _():
            for k in range(8):
                margin_copy(c, k, 0).start()

        @pl.when(has_down)
        def _():
            for k in range(8):
                margin_copy(c, k, 1).start()

        placed_share(c, p, share)
        return 0

    def source_arrived(c):
        for k, (dx, dz) in enumerate(PEERS):
            ag_copy(c, k).wait_recv()
            placed_share(c, pole_at(4 - dx, dz), decoded(agr[c, k], agrp[c, k]))

        @pl.when(has_up)
        def _():
            for k in range(8):
                margin_copy(c, k, 1).wait_recv()

        @pl.when(has_down)
        def _():
            for k in range(8):
                margin_copy(c, k, 0).wait_recv()

    def first_sweep(c, _):
        wait_recv_both(halo_copy, c)
        sweep_one(0, c)
        residual(0, c)
        return 0

    lax.fori_loop(0, chunks, first_sweep, 0)
    lax.fori_loop(0, chunks, inner_product, 0)

    def second_sweep(c, _):
        finish(0, c)
        return 0

    lax.fori_loop(0, chunks, second_sweep, 0)
    lax.fori_loop(0, chunks, next_source, 0)

    def first_sweep_again(c, _):
        source_arrived(c)
        sweep_one(1, c)
        residual(1, c)
        inner_product(c, 0)
        return 0

    lax.fori_loop(0, chunks, first_sweep_again, 0)

    def second_sweep_again(c, _):
        finish(1, c)
        return 0

    lax.fori_loop(0, chunks, second_sweep_again, 0)
    for c in range(chunks):
        out_ref[:, c * N : c * N + N] = summed(1, c)

    def drain(c, _):
        wait_send_both(halo_copy, c)
        for t in range(2):
            wait_send_both(edge_copy, t, c)
            for k in range(7):
                rs_copy(t, c, k).wait_send()
        for k in range(7):
            ag_copy(c, k).wait_send()

        @pl.when(has_up)
        def _():
            for k in range(8):
                margin_copy(c, k, 0).wait_send()

        @pl.when(has_down)
        def _():
            for k in range(8):
                margin_copy(c, k, 1).wait_send()

        return 0

    lax.fori_loop(0, chunks, drain, 0)


def shards(state, conductivity, pole_shift, pole_weight, order_list, inverse):
    rows, columns = state.shape
    chunks = columns // N
    vmem = pl.BlockSpec(memory_space=pltpu.VMEM)
    smem = pl.BlockSpec(memory_space=pltpu.SMEM)
    anywhere = pl.BlockSpec(memory_space=pl.ANY)
    dma = pltpu.SemaphoreType.DMA

    def body(*refs):
        kernel(chunks, *refs)

    return pl.pallas_call(
        body,
        out_shape=jax.ShapeDtypeStruct((rows // 8, columns), F32),
        in_specs=[vmem, vmem, smem, smem, anywhere, anywhere],
        out_specs=vmem,
        scratch_shapes=[
            pltpu.VMEM((768, 2048), BF16),
            pltpu.VMEM((chunks, 768, N), F32),
            pltpu.VMEM((768, N), F32),
            pltpu.VMEM((1536, 1024), BF16),
            pltpu.VMEM((2, chunks, 1024, N), BF16),
            pltpu.VMEM((chunks, 2, H, N), BF16),
            pltpu.VMEM((chunks, 2, 784, N), F32),
            pltpu.VMEM((chunks, 768, N), F32),
            pltpu.VMEM((chunks, 2, 2, H, N), F32),
            pltpu.VMEM((2, chunks, 2, 4, H, N), I16),
            pltpu.VMEM((2, chunks, 2, 4, H, N), I16),
            pltpu.VMEM((2, chunks, 2, 4, N), F32),
            pltpu.VMEM((2, chunks, 2, 4, N), F32),
            pltpu.VMEM((chunks, 1024, 2 * N), BF16),
            pltpu.VMEM((2, chunks, 8, 96, N), I16),
            pltpu.VMEM((2, chunks, 7, 96, N), I16),
            pltpu.VMEM((2, chunks, 1, N), F32),
            pltpu.VMEM((2, chunks, 7, 1, N), F32),
            pltpu.VMEM((chunks, 96, N), I16),
            pltpu.VMEM((chunks, 7, 96, N), I16),
            pltpu.VMEM((chunks, 1, N), F32),
            pltpu.VMEM((chunks, 7, 1, N), F32),
            pltpu.VMEM((chunks, 2, 16, N), BF16),
            dma((chunks + 1,)),
            dma((chunks, 2)),
            dma((chunks, 2)),
            dma((2, chunks, 2, 2)),
            dma((2, chunks, 2, 2)),
            dma((2, chunks, 7, 2)),
            dma((2, chunks, 7, 2)),
            dma((chunks, 7, 2)),
            dma((chunks, 7, 2)),
            dma((chunks, 8, 2)),
            dma((chunks, 8, 2)),
        ],
        compiler_params=pltpu.CompilerParams(
            collective_id=0, has_side_effects=True, vmem_limit_bytes=58 << 20
        ),
    )(order_list, conductivity.reshape(1, rows), pole_shift, pole_weight, state, inverse)


def solution(mesh):
    placed = (
        P("sub", None),
        P("sub"),
        P("pole", None),
        P("pole", None),
        P("sub", None),
        P("pole", "sub", None),
    )
    return jax.shard_map(
        shards, mesh=mesh, in_specs=placed, out_specs=P(("sub", "pole"), None), check_vma=False
    )
```

time: 237 us -> 71.6 us (0.30)
  the two profiles are of different devices: /device:TPU:32 before, /device:TPU:0 now
where the time goes in v1:
time: 71.6 us; the launch traced here: 70.5 us
  Pallas kernels  67.7 us (95%)
  local copies, waits for them, and re-layouts  2.88 us (4%)
    pallas_call x1, Pallas kernels, shards(): pl.pallas_call(body, out_shape=jax.ShapeDtypeStruct((rows // 8, columns),...  67.7 us
    unnamed x1, local copies, waits for them, and re-layouts  1.62 us

profile of v1, /device:TPU:0, one launch (start us, length us, event | category | flops | bytes accessed | tf_op | source)
XLA Modules:
  0.0 70.5 jit_solution(9468818898750057862)
XLA Ops:
  0.0 1.3 %reshape.3.refs_1_ = f32[1,768]{1,0:T(1,128)} reshape(f32[768]{0:T(1024)} %param.7) | data formatting | bytes 6144 | tf_op jit(solution)/shard_map/reshape | solution.py:496
  1.3 67.7 %shard_map.64 = f32[96,512]{1,0:T(8,128)} custom-call(s32[1,1024]{1,0:T(1,128)} %refs_0_.1, f32[1,768]{1,0:T(1,128)} %reshape.3.refs_1_, f32[1,2]{1,0:T(1,128)} %refs_2_.1, f32[1,2]{1,0:T(1,128)} %refs_3_.1, f32[768,512]{1,0:T(8,128)} %refs_4_.1, bf16[1,768,2048]{2,1,0:T(8,128)(2,1)} %refs_5_.1), custom_call_target="tpu_custom_call" | custom-call | tf_op jit(solution)/shard_map/pallas_call | solution.py:452
  68.9 1.6 %copy.8 = f32[96,512]{1,0:T(8,128)} copy(f32[96,512]{1,0:T(8,128)} %shard_map.64) | data formatting | bytes 393216

commit v2 on v1

v2 whole, which is shorter than its diff:
```python
import jax
import jax.numpy as jnp
from jax import lax
from jax.experimental import pallas as pl
from jax.experimental.pallas import tpu as pltpu
from jax.sharding import PartitionSpec as P

MESH = pl.DeviceIdType.MESH
F32 = jnp.float32
BF16 = jnp.bfloat16
H = 128
N = 128
PAIR = 2 * N
PEERS = ((2, 1), (1, 1), (3, 1), (2, 0), (0, 1), (1, 0), (3, 0))
I16 = jnp.int16
TOP = 32767.0


def rounded(x):
    return x.astype(BF16)


def coded(v, peak):
    return jnp.round(v * (TOP / peak)).astype(jnp.int32).astype(I16)


def peak_of(v):
    return jnp.maximum(jnp.max(jnp.abs(v), axis=0, keepdims=True), 1e-30)


def decoded(q, peak):
    return q.astype(jnp.int32).astype(F32) * (peak * (1.0 / TOP))


def kernel(
    chunks, order_ref, cond_ref, shift_ref, weight_ref, state_hbm, inv_hbm, out_ref,
    g_in, st, cb, gp, e1, hs, x, acc, rp, p1s, p1r, p1sp, p1rp, e2, rss, rsr, rssp, rsrp,
    ags, agr, agsp, agrp, res,
    in_sem, halo_ss, halo_rs, p1_ss, p1_rs, rs_ss, rs_rs, ag_ss, ag_rs,
):
    pairs = chunks // 2
    s = lax.axis_index("sub")
    p = lax.axis_index("pole")
    px, pz = p // 2, lax.rem(p, 2)
    subs = lax.axis_size("sub")
    has_up, has_down = s > 0, s < subs - 1
    up, down = lax.rem(s + subs - 1, subs), lax.rem(s + 1, subs)

    def pole_at(dx, dz):
        return lax.rem(px + dx, 4) * 2 + lax.rem(pz + dz, 2)

    def remote(src, dst, send_sem, recv_sem, sub, pole):
        return pltpu.make_async_remote_copy(
            src_ref=src, dst_ref=dst, send_sem=send_sem, recv_sem=recv_sem,
            device_id=(sub, pole), device_id_type=MESH,
        )

    state_in = [
        pltpu.make_async_copy(state_hbm.at[:, pl.ds(c * N, N)], st.at[c], in_sem.at[0])
        for c in range(chunks)
    ]
    for copy in state_in:
        copy.start()
    g_copy = pltpu.make_async_copy(inv_hbm.at[0], g_in, in_sem.at[1])
    g_copy.start()

    barrier = pltpu.get_barrier_semaphore()
    for dx, dz in PEERS:
        pl.semaphore_signal(barrier, inc=1, device_id=(s, pole_at(dx, dz)), device_id_type=MESH)
    pl.semaphore_signal(barrier, inc=1, device_id=(up, p), device_id_type=MESH)
    pl.semaphore_signal(barrier, inc=1, device_id=(down, p), device_id_type=MESH)

    shift_re, shift_im = shift_ref[0, 0], shift_ref[0, 1]
    w_re, w_im = 2.0 * weight_ref[0, 0], 2.0 * weight_ref[0, 1]

    for b in range(6):
        row = cond_ref[128 * b : 128 * b + 128]
        cb[128 * b : 128 * b + 128, :] = jnp.broadcast_to(row[None, :], (128, 128)).T

    for c in range(chunks):
        for d in range(2):
            x[c, d, 0:8, :] = jnp.zeros((8, N), F32)
            x[c, d, 776:784, :] = jnp.zeros((8, N), F32)

    @pl.when(jnp.logical_not(has_up))
    def _():
        for t in range(2):
            for j in range(pairs):
                e1[t, j, 768:896, :] = jnp.zeros((H, PAIR), BF16)
            for c in range(chunks):
                p1r[0, t, c] = jnp.zeros((4, H, N), I16)
                p1rp[0, t, c] = jnp.zeros((4, N), F32)

    @pl.when(jnp.logical_not(has_down))
    def _():
        for t in range(2):
            for j in range(pairs):
                e1[t, j, 896:1024, :] = jnp.zeros((H, PAIR), BF16)
            for c in range(chunks):
                p1r[1, t, c] = jnp.zeros((4, H, N), I16)
                p1rp[1, t, c] = jnp.zeros((4, N), F32)

    pltpu.make_async_copy(st, st, in_sem.at[0]).wait()
    for c in range(chunks):
        j, to = c // 2, slice(N * (c % 2), N * (c % 2) + N)
        src = cb[...] * st[c]
        st[c] = src
        e1[0, j, 0:512, to] = rounded(src[128:640])
        top = rounded(src[0:128])
        bottom = rounded(src[640:768])
        hs[0, 0, j, :, to] = top
        hs[1, 0, j, :, to] = bottom
        for q in range(8):
            e1[0, j, 512 + 32 * q : 528 + 32 * q, to] = top[16 * q : 16 * q + 16]
            e1[0, j, 528 + 32 * q : 544 + 32 * q, to] = bottom[16 * q : 16 * q + 16]

    def halo_copy(t, j, d):
        return remote(
            hs.at[d, t, j], e1.at[t, j, pl.ds(896 - 128 * d, H)], halo_ss.at[d], halo_rs.at[t, j, d],
            down if d else up, p,
        )

    class Several:
        def __init__(self, *copies):
            self.copies = copies

        def start(self):
            for copy in self.copies:
                copy.start()

        def wait_recv(self):
            for copy in self.copies:
                copy.wait_recv()

        def wait_send(self):
            for copy in self.copies:
                copy.wait_send()

    def edge_copy(t, c, d):
        to = down if d else up
        return Several(
            remote(p1sp.at[d, t, c], p1rp.at[1 - d, t, c], p1_ss.at[d, 1], p1_rs.at[t, c, d, 1], to, p),
            remote(p1s.at[d, t, c], p1r.at[1 - d, t, c], p1_ss.at[d, 0], p1_rs.at[t, c, d, 0], to, p),
        )

    def start_both(make, *args):
        @pl.when(has_up)
        def _():
            make(*args, 0).start()

        @pl.when(has_down)
        def _():
            make(*args, 1).start()

    def wait_recv_both(make, *args):
        @pl.when(has_up)
        def _():
            make(*args, 1).wait_recv()

        @pl.when(has_down)
        def _():
            make(*args, 0).wait_recv()

    g_copy.wait()
    order = order_ref[...]

    def extended_row(base, count):
        return lax.broadcasted_iota(jnp.int32, (count, 1), 0) + base

    for blk in range(4):
        if blk == 2:
            pl.semaphore_wait(barrier, 9)
            for j in range(pairs):
                start_both(halo_copy, 0, j)
        if blk < 2:
            rows = extended_row(256 + 256 * blk, 256)
        elif blk == 2:
            rows = jnp.concatenate(
                [extended_row(b + 16 * q, 16) for q in range(8) for b in (128, 768)], axis=0
            )
        else:
            rows = jnp.concatenate([extended_row(0, 128), extended_row(896, 128)], axis=0)
        hot = jnp.where(rows == order, 1.0, 0.0).astype(BF16)
        at = 256 * blk
        for m in range(2):
            r0 = 384 * m
            re = lax.dot_general(
                g_in[r0 : r0 + 384, 0:1024], hot, (((1,), (1,)), ((), ())), preferred_element_type=F32
            )
            im = lax.dot_general(
                g_in[r0 : r0 + 384, 1024:2048], hot, (((1,), (1,)), ((), ())), preferred_element_type=F32
            )
            gp[r0 : r0 + 384, at : at + 256] = rounded(re)
            gp[768 + r0 : 768 + r0 + 384, at : at + 256] = rounded(im)

    def own_sweep(t, j):
        y = jnp.dot(gp[:, 0:768], e1[t, j, 0:768, :], preferred_element_type=F32)
        for i in range(2):
            for d in range(2):
                x[2 * j + i, d, 8:776, :] = y[768 * d : 768 * d + 768, N * i : N * i + N]

    def margin_sweep(t, j):
        y = jnp.dot(gp[:, 768:1024], e1[t, j, 768:1024, :], preferred_element_type=F32)
        for i in range(2):
            for d in range(2):
                x[2 * j + i, d, 8:776, :] += y[768 * d : 768 * d + 768, N * i : N * i + N]

    def residual(t, c):
        for b in (0, 5, 1, 2, 3, 4):
            at = 8 + 128 * b

            def lap(d):
                v = (
                    4.0 * x[c, d, at : at + 128, :]
                    - x[c, d, at - 1 : at + 127, :]
                    - x[c, d, at + 1 : at + 129, :]
                )
                if b > 0:
                    v = v - x[c, d, at - 128 : at, :]
                if b < 5:
                    v = v - x[c, d, at + 128 : at + 256, :]
                return v

            xr = x[c, 0, at : at + 128, :]
            xi = x[c, 1, at : at + 128, :]
            sigma = cb[128 * b : 128 * b + 128, :]
            src = st[c, 128 * b : 128 * b + 128, :]
            rr = src - lap(0) - sigma * (shift_re * xr - shift_im * xi)
            ri = -lap(1) - sigma * (shift_im * xr + shift_re * xi)
            acc[c, 128 * b : 128 * b + 128, :] = w_re * xr - w_im * xi
            if 0 < b < 5:
                e2[c, 128 * (b - 1) : 128 * b, 0:N] = rounded(rr)
                e2[c, 128 * (b - 1) : 128 * b, N : 2 * N] = rounded(ri)
            else:
                d = 0 if b == 0 else 1
                rp[c, d, 0] = rr
                rp[c, d, 1] = ri
                for i, v in enumerate((xr, xi, rr, ri)):
                    peak = peak_of(v)
                    p1sp[d, t, c, i : i + 1, :] = peak
                    p1s[d, t, c, i] = coded(v, peak)
        start_both(edge_copy, t, c)

    def weighted(y):
        re = y[:768, 0:N] - y[768:, N : 2 * N]
        im = y[:768, N : 2 * N] + y[768:, 0:N]
        return w_re * re - w_im * im

    def inner_product(c, _):
        acc[c] += weighted(jnp.dot(gp[:, 0:512], e2[c, 0:512, :], preferred_element_type=F32))
        return 0

    row_of = lax.broadcasted_iota(jnp.int32, (H, 1), 0)
    up_on = jnp.where(has_up, 1.0, 0.0).astype(F32)
    down_on = jnp.where(has_down, 1.0, 0.0).astype(F32)

    def rs_copy(t, c, k):
        q = pole_at(*PEERS[k])
        return Several(
            remote(rssp.at[t, c], rsrp.at[t, c, k], rs_ss.at[1], rs_rs.at[t, c, 1], s, q),
            remote(rss.at[t, c, q], rsr.at[t, c, k], rs_ss.at[0], rs_rs.at[t, c, 0], s, q),
        )

    def finish(t, c):
        wait_recv_both(edge_copy, t, c)
        for d in range(2):
            base = 512
            to = slice(N * d, N * d + N)

            def came(side, i):
                return decoded(p1r[side, t, c, i], p1rp[side, t, c, i : i + 1, :])

            above, below = came(0, d), came(1, d)
            top = rp[c, 0, d] + above + jnp.where(row_of == 0, above[127:128], 0.0)
            bottom = rp[c, 1, d] + below + jnp.where(row_of == 127, below[0:1], 0.0)
            top, bottom = rounded(top), rounded(bottom)
            for q in range(8):
                e2[c, base + 32 * q : base + 32 * q + 16, to] = top[16 * q : 16 * q + 16]
                e2[c, base + 32 * q + 16 : base + 32 * q + 32, to] = bottom[16 * q : 16 * q + 16]
            first = x[c, d, 8:136, :]
            final = x[c, d, 648:776, :]
            over = came(0, 2 + d) + first + jnp.where(row_of == 127, first[0:1], 0.0)
            under = came(1, 2 + d) + final + jnp.where(row_of == 0, final[127:128], 0.0)
            e2[c, base + 256 : base + 384, to] = rounded(up_on * over)
            e2[c, base + 384 : base + 512, to] = rounded(down_on * under)
        total = acc[c] + weighted(jnp.dot(gp[:, 512:1024], e2[c, 512:1024, :], preferred_element_type=F32))
        peak = peak_of(total)
        rssp[t, c] = peak
        total = coded(total, peak)
        for q in range(8):
            if t == 0:
                rss[t, c, q, 0:64, :] = total[128 + 64 * q : 192 + 64 * q]
                rss[t, c, q, 64:80, :] = total[16 * q : 16 * q + 16]
                rss[t, c, q, 80:96, :] = total[640 + 16 * q : 656 + 16 * q]
            else:
                rss[t, c, q] = total[96 * q : 96 * q + 96]
        for k in range(7):
            rs_copy(t, c, k).start()

    def all_came(ref, sem):
        pltpu.make_async_copy(ref, ref, sem).wait()

    def summed(t, c):
        total = decoded(rss[t, c, p], rssp[t, c])
        all_came(rsrp.at[t, c], rs_rs.at[t, c, 1])
        all_came(rsr.at[t, c], rs_rs.at[t, c, 0])
        for k in range(7):
            total = total + decoded(rsr[t, c, k], rsrp[t, c, k])
        return total

    def ag_copy(c, k):
        q = pole_at(*PEERS[k])
        return Several(
            remote(agsp.at[c], agrp.at[c, k], ag_ss.at[1], ag_rs.at[c, 1], s, q),
            remote(ags.at[c], agr.at[c, k], ag_ss.at[0], ag_rs.at[c, 0], s, q),
        )

    def placed_share(j, i, q, share):
        c, to = 2 * j + i, slice(N * i, N * i + N)
        st[c, pl.ds(pl.multiple_of(128 + 64 * q, 64), 64), :] = share[0:64]
        st[c, pl.ds(pl.multiple_of(16 * q, 16), 16), :] = share[64:80]
        st[c, pl.ds(pl.multiple_of(640 + 16 * q, 16), 16), :] = share[80:96]
        share = rounded(share)
        e1[1, j, pl.ds(pl.multiple_of(64 * q, 64), 64), to] = share[0:64]
        e1[1, j, pl.ds(pl.multiple_of(512 + 32 * q, 32), 32), to] = share[64:96]
        hs[0, 1, j, pl.ds(pl.multiple_of(16 * q, 16), 16), to] = share[64:80]
        hs[1, 1, j, pl.ds(pl.multiple_of(16 * q, 16), 16), to] = share[80:96]

    def next_source(j, i):
        c = 2 * j + i
        total = summed(0, c)
        sigma = jnp.concatenate(
            [
                cb[pl.ds(pl.multiple_of(128 + 64 * p, 64), 64), :],
                cb[pl.ds(pl.multiple_of(16 * p, 16), 16), :],
                cb[pl.ds(pl.multiple_of(640 + 16 * p, 16), 16), :],
            ],
            axis=0,
        )
        share = sigma * total
        peak = peak_of(share)
        agsp[c] = peak
        ags[c] = coded(share, peak)
        for k in range(7):
            ag_copy(c, k).start()
        placed_share(j, i, p, share)

    def source_arrived(j):
        for i in range(2):
            c = 2 * j + i
            all_came(agrp.at[c], ag_rs.at[c, 1])
            all_came(agr.at[c], ag_rs.at[c, 0])
            for k, (dx, dz) in enumerate(PEERS):
                placed_share(j, i, pole_at(4 - dx, dz), decoded(agr[c, k], agrp[c, k]))
        start_both(halo_copy, 1, j)

    def over_pairs(step, *args):
        def body(j, _):
            step(*args, j)
            return 0

        lax.fori_loop(0, pairs, body, 0)

    def first_sweep(t, j):
        wait_recv_both(halo_copy, t, j)
        margin_sweep(t, j)

        def body(i, _):
            residual(t, 2 * j + i)
            return 0

        lax.fori_loop(0, 2, body, 0)

    def second_sweep(t):
        def body(c, _):
            finish(t, c)
            return 0

        lax.fori_loop(0, chunks, inner_product, 0)
        lax.fori_loop(0, chunks, body, 0)

    def both_next(j):
        for i in range(2):
            next_source(j, i)

    def source_in(j):
        source_arrived(j)
        own_sweep(1, j)

    over_pairs(own_sweep, 0)
    over_pairs(first_sweep, 0)
    second_sweep(0)
    over_pairs(both_next)
    over_pairs(source_in)
    over_pairs(first_sweep, 1)
    second_sweep(1)

    for c in range(chunks):
        res[:, c * N : c * N + N] = summed(1, c)
        pltpu.make_async_copy(
            res.at[:, pl.ds(c * N, N)], out_ref.at[:, pl.ds(c * N, N)], in_sem.at[0]
        ).start()

    all_came(rsr, rs_ss.at[0])
    all_came(rsrp, rs_ss.at[1])
    all_came(agr, ag_ss.at[0])
    all_came(agrp, ag_ss.at[1])

    def all_left(d):
        all_came(hs.at[d], halo_ss.at[d])
        all_came(p1s.at[d], p1_ss.at[d, 0])
        all_came(p1sp.at[d], p1_ss.at[d, 1])

    @pl.when(has_up)
    def _():
        all_left(0)

    @pl.when(has_down)
    def _():
        all_left(1)

    all_came(res, in_sem.at[0])


def shards(state, conductivity, pole_shift, pole_weight, order_list, inverse):
    rows, columns = state.shape
    chunks = columns // N
    vmem = pl.BlockSpec(memory_space=pltpu.VMEM)
    smem = pl.BlockSpec(memory_space=pltpu.SMEM)
    anywhere = pl.BlockSpec(memory_space=pl.ANY)
    dma = pltpu.SemaphoreType.DMA

    def body(*refs):
        kernel(chunks, *refs)

    return pl.pallas_call(
        body,
        out_shape=jax.ShapeDtypeStruct((rows // 8, columns), F32),
        in_specs=[vmem, vmem, smem, smem, anywhere, anywhere],
        out_specs=anywhere,
        scratch_shapes=[
            pltpu.VMEM((768, 2048), BF16),
            pltpu.VMEM((chunks, 768, N), F32),
            pltpu.VMEM((768, N), F32),
            pltpu.VMEM((1536, 1024), BF16),
            pltpu.VMEM((2, chunks // 2, 1024, PAIR), BF16),
            pltpu.VMEM((2, 2, chunks // 2, H, PAIR), BF16),
            pltpu.VMEM((chunks, 2, 784, N), F32),
            pltpu.VMEM((chunks, 768, N), F32),
            pltpu.VMEM((chunks, 2, 2, H, N), F32),
            pltpu.VMEM((2, 2, chunks, 4, H, N), I16),
            pltpu.VMEM((2, 2, chunks, 4, H, N), I16),
            pltpu.VMEM((2, 2, chunks, 4, N), F32),
            pltpu.VMEM((2, 2, chunks, 4, N), F32),
            pltpu.VMEM((chunks, 1024, 2 * N), BF16),
            pltpu.VMEM((2, chunks, 8, 96, N), I16),
            pltpu.VMEM((2, chunks, 7, 96, N), I16),
            pltpu.VMEM((2, chunks, 1, N), F32),
            pltpu.VMEM((2, chunks, 7, 1, N), F32),
            pltpu.VMEM((chunks, 96, N), I16),
            pltpu.VMEM((chunks, 7, 96, N), I16),
            pltpu.VMEM((chunks, 1, N), F32),
            pltpu.VMEM((chunks, 7, 1, N), F32),
            pltpu.VMEM((96, chunks * N), F32),
            dma((2,)),
            dma((2,)),
            dma((2, chunks // 2, 2)),
            dma((2, 2)),
            dma((2, chunks, 2, 2)),
            dma((2,)),
            dma((2, chunks, 2)),
            dma((2,)),
            dma((chunks, 2)),
        ],
        compiler_params=pltpu.CompilerParams(
            collective_id=0, has_side_effects=True, vmem_limit_bytes=58 << 20
        ),
    )(order_list, conductivity, pole_shift, pole_weight, state, inverse)


def solution(mesh):
    placed = (
        P("sub", None),
        P("sub"),
        P("pole", None),
        P("pole", None),
        P("sub", None),
        P("pole", "sub", None),
    )
    return jax.shard_map(
        shards, mesh=mesh, in_specs=placed, out_specs=P(("sub", "pole"), None), check_vma=False
    )
```

time: 71.6 us -> 63.6 us (0.89); the launches traced: 70.5 us -> 63.4 us
  Pallas kernels: 67.7 us -> 61.8 us
  local copies, waits for them, and re-layouts: 2.88 us -> 1.62 us
    pallas_call x1, Pallas kernels: 67.7 us -> 61.8 us  [shards(): pl.pallas_call(body, out_shape=jax.ShapeDtypeStruct((rows // 8, columns),...]
    reshape x1 -> x0, local copies, waits for them, and re-layouts: 1.27 us -> none  [shards(): conductivity.reshape(1, rows)]
where the time goes in v2:
time: 63.6 us; the launch traced here: 63.4 us
  Pallas kernels  61.8 us (97%)
  local copies, waits for them, and re-layouts  1.62 us (3%)
    pallas_call x1, Pallas kernels, shards(): pl.pallas_call(body, out_shape=jax.ShapeDtypeStruct((rows // 8, columns),...  61.8 us
    unnamed x1, local copies, waits for them, and re-layouts  1.62 us

profile of v2, /device:TPU:0, one launch (start us, length us, event | category | flops | bytes accessed | tf_op | source)
XLA Modules:
  0.0 63.4 jit_solution(8682496307460503149)
XLA Ops:
  0.0 61.8 %shard_map.64 = f32[96,512]{1,0:T(8,128)} custom-call(s32[1,1024]{1,0:T(1,128)} %refs_0_.1, f32[768]{0:T(1024)} %refs_1_.1, f32[1,2]{1,0:T(1,128)} %refs_2_.1, f32[1,2]{1,0:T(1,128)} %refs_3_.1, f32[768,512]{1,0:T(8,128)} %refs_4_.1, bf16[1,768,2048]{2,1,0:T(8,128)(2,1)} %refs_5_.1), custom_call_target="tpu_custom_call" | custom-call | tf_op jit(solution)/shard_map/pallas_call | solution.py:436
  61.8 1.6 %copy.8 = f32[96,512]{1,0:T(8,128)} copy(f32[96,512]{1,0:T(8,128)} %shard_map.64) | data formatting | bytes 393216

commit v3 on v2

--- a/solution.py
+++ b/solution.py
@@ -12,6 +12,7 @@
 N = 128
 PAIR = 2 * N
 PEERS = ((2, 1), (1, 1), (3, 1), (2, 0), (0, 1), (1, 0), (3, 0))
+EVERY = PEERS + ((0, 0),)
 I16 = jnp.int16
 TOP = 32767.0
 
@@ -35,8 +36,8 @@
 def kernel(
     chunks, order_ref, cond_ref, shift_ref, weight_ref, state_hbm, inv_hbm, out_ref,
     g_in, st, cb, gp, e1, hs, x, acc, rp, p1s, p1r, p1sp, p1rp, e2, rss, rsr, rssp, rsrp,
-    ags, agr, agsp, agrp, res,
-    in_sem, halo_ss, halo_rs, p1_ss, p1_rs, rs_ss, rs_rs, ag_ss, ag_rs,
+    ags, agm, age, agsp, agrp, nbs, res,
+    in_sem, halo_ss, halo_rs, p1_ss, p1_rs, rs_ss, rs_rs, ag_ss, ag_rs, nb_ss, nb_rs,
 ):
     pairs = chunks // 2
     s = lax.axis_index("sub")
@@ -61,8 +62,9 @@
     ]
     for copy in state_in:
         copy.start()
-    g_copy = pltpu.make_async_copy(inv_hbm.at[0], g_in, in_sem.at[1])
-    g_copy.start()
+    for b in range(4):
+        part = pl.ds(192 * b, 192)
+        pltpu.make_async_copy(inv_hbm.at[0, part], g_in.at[part], in_sem.at[1]).start()
 
     barrier = pltpu.get_barrier_semaphore()
     for dx, dz in PEERS:
@@ -108,15 +110,15 @@
         e1[0, j, 0:512, to] = rounded(src[128:640])
         top = rounded(src[0:128])
         bottom = rounded(src[640:768])
-        hs[0, 0, j, :, to] = top
-        hs[1, 0, j, :, to] = bottom
+        hs[0, j, :, to] = top
+        hs[1, j, :, to] = bottom
         for q in range(8):
             e1[0, j, 512 + 32 * q : 528 + 32 * q, to] = top[16 * q : 16 * q + 16]
             e1[0, j, 528 + 32 * q : 544 + 32 * q, to] = bottom[16 * q : 16 * q + 16]
 
     def halo_copy(t, j, d):
         return remote(
-            hs.at[d, t, j], e1.at[t, j, pl.ds(896 - 128 * d, H)], halo_ss.at[d], halo_rs.at[t, j, d],
+            hs.at[d, pairs * t + j], e1.at[t, j, pl.ds(896 - 128 * d, H)], halo_ss.at[d], halo_rs.at[t, j, d],
             down if d else up, p,
         )
 
@@ -161,17 +163,17 @@
         def _():
             make(*args, 0).wait_recv()
 
-    g_copy.wait()
+    pl.semaphore_wait(barrier, 9)
+    for j in range(pairs):
+        start_both(halo_copy, 0, j)
+
+    pltpu.make_async_copy(g_in, g_in, in_sem.at[1]).wait()
     order = order_ref[...]
 
     def extended_row(base, count):
         return lax.broadcasted_iota(jnp.int32, (count, 1), 0) + base
 
     for blk in range(4):
-        if blk == 2:
-            pl.semaphore_wait(barrier, 9)
-            for j in range(pairs):
-                start_both(halo_copy, 0, j)
         if blk < 2:
             rows = extended_row(256 + 256 * blk, 256)
         elif blk == 2:
@@ -308,23 +310,65 @@
             total = total + decoded(rsr[t, c, k], rsrp[t, c, k])
         return total
 
-    def ag_copy(c, k):
+    def ag_copy(c, k, part):
         q = pole_at(*PEERS[k])
+        if part:
+            return remote(ags.at[c, pl.ds(0, 64)], agm.at[c, k], ag_ss.at[0], ag_rs.at[c, 0], s, q)
         return Several(
-            remote(agsp.at[c], agrp.at[c, k], ag_ss.at[1], ag_rs.at[c, 1], s, q),
-            remote(ags.at[c], agr.at[c, k], ag_ss.at[0], ag_rs.at[c, 0], s, q),
-        )
-
-    def placed_share(j, i, q, share):
+            remote(agsp.at[c], agrp.at[c, k], ag_ss.at[2], ag_rs.at[c, 2], s, q),
+            remote(ags.at[c, pl.ds(64, 32)], age.at[c, k], ag_ss.at[1], ag_rs.at[c, 1], s, q),
+        )
+
+    def placed_middle(j, i, q, share):
+        to = slice(N * i, N * i + N)
+        st[2 * j + i, pl.ds(pl.multiple_of(128 + 64 * q, 64), 64), :] = share
+        e1[1, j, pl.ds(pl.multiple_of(64 * q, 64), 64), to] = rounded(share)
+
+    def placed_edges(j, i, q, share):
         c, to = 2 * j + i, slice(N * i, N * i + N)
-        st[c, pl.ds(pl.multiple_of(128 + 64 * q, 64), 64), :] = share[0:64]
-        st[c, pl.ds(pl.multiple_of(16 * q, 16), 16), :] = share[64:80]
-        st[c, pl.ds(pl.multiple_of(640 + 16 * q, 16), 16), :] = share[80:96]
+        st[c, pl.ds(pl.multiple_of(16 * q, 16), 16), :] = share[0:16]
+        st[c, pl.ds(pl.multiple_of(640 + 16 * q, 16), 16), :] = share[16:32]
         share = rounded(share)
-        e1[1, j, pl.ds(pl.multiple_of(64 * q, 64), 64), to] = share[0:64]
-        e1[1, j, pl.ds(pl.multiple_of(512 + 32 * q, 32), 32), to] = share[64:96]
-        hs[0, 1, j, pl.ds(pl.multiple_of(16 * q, 16), 16), to] = share[64:80]
-        hs[1, 1, j, pl.ds(pl.multiple_of(16 * q, 16), 16), to] = share[80:96]
+        e1[1, j, pl.ds(pl.multiple_of(512 + 32 * q, 32), 32), to] = share
+
+        @pl.when(j < pairs - 1)
+        def _():
+            hs[0, pairs + j, pl.ds(pl.multiple_of(16 * q, 16), 16), to] = share[0:16]
+            hs[1, pairs + j, pl.ds(pl.multiple_of(16 * q, 16), 16), to] = share[16:32]
+
+    last = pairs - 1
+
+    def margin_copy(i, k, d):
+        dst = e1.at[1, last, pl.ds(pl.multiple_of(896 - 128 * d + 16 * p, 16), 16), pl.ds(N * i, N)]
+        return remote(
+            nbs.at[i, d], dst, nb_ss.at[d], nb_rs.at[i, d], down if d else up, pole_at(*EVERY[k])
+        )
+
+    def margins_of(i, edges):
+        for d in range(2):
+            nbs[i, d] = edges[16 * d : 16 * d + 16]
+
+        @pl.when(has_up)
+        def _():
+            for k in range(8):
+                margin_copy(i, k, 0).start()
+
+        @pl.when(has_down)
+        def _():
+            for k in range(8):
+                margin_copy(i, k, 1).start()
+
+    def margins_in():
+        for i in range(2):
+            to = pl.ds(N * i, N)
+
+            @pl.when(has_up)
+            def _():
+                all_came(e1.at[1, last, pl.ds(768, H), to], nb_rs.at[i, 1])
+
+            @pl.when(has_down)
+            def _():
+                all_came(e1.at[1, last, pl.ds(896, H), to], nb_rs.at[i, 0])
 
     def next_source(j, i):
         c = 2 * j + i
@@ -342,17 +386,35 @@
         agsp[c] = peak
         ags[c] = coded(share, peak)
         for k in range(7):
-            ag_copy(c, k).start()
-        placed_share(j, i, p, share)
-
-    def source_arrived(j):
+            ag_copy(c, k, 0).start()
+
+        @pl.when(j == last)
+        def _():
+            margins_of(i, rounded(share[64:96]))
+
+        for k in range(7):
+            ag_copy(c, k, 1).start()
+        placed_middle(j, i, p, share[0:64])
+        placed_edges(j, i, p, share[64:96])
+
+    def edges_in(j):
         for i in range(2):
             c = 2 * j + i
-            all_came(agrp.at[c], ag_rs.at[c, 1])
-            all_came(agr.at[c], ag_rs.at[c, 0])
+            all_came(agrp.at[c], ag_rs.at[c, 2])
+            all_came(age.at[c], ag_rs.at[c, 1])
             for k, (dx, dz) in enumerate(PEERS):
-                placed_share(j, i, pole_at(4 - dx, dz), decoded(agr[c, k], agrp[c, k]))
-        start_both(halo_copy, 1, j)
+                placed_edges(j, i, pole_at(4 - dx, dz), decoded(age[c, k], agrp[c, k]))
+
+        @pl.when(j < last)
+        def _():
+            start_both(halo_copy, 1, j)
+
+    def middle_in(j):
+        for i in range(2):
+            c = 2 * j + i
+            all_came(agm.at[c], ag_rs.at[c, 0])
+            for k, (dx, dz) in enumerate(PEERS):
+                placed_middle(j, i, pole_at(4 - dx, dz), decoded(agm[c, k], agrp[c, k]))
 
     def over_pairs(step, *args):
         def body(j, _):
@@ -362,7 +424,18 @@
         lax.fori_loop(0, pairs, body, 0)
 
     def first_sweep(t, j):
-        wait_recv_both(halo_copy, t, j)
+        if t == 0:
+            wait_recv_both(halo_copy, t, j)
+        else:
+
+            @pl.when(j < last)
+            def _():
+                wait_recv_both(halo_copy, 1, j)
+
+            @pl.when(j == last)
+            def _():
+                margins_in()
+
         margin_sweep(t, j)
 
         def body(i, _):
@@ -371,28 +444,52 @@
 
         lax.fori_loop(0, 2, body, 0)
 
-    def second_sweep(t):
-        def body(c, _):
-            finish(t, c)
-            return 0
-
-        lax.fori_loop(0, chunks, inner_product, 0)
-        lax.fori_loop(0, chunks, body, 0)
+    def opening(j):
+        own_sweep(0, j)
+        first_sweep(0, j)
+
+    def opening_again(j):
+        middle_in(j)
+        own_sweep(1, j)
+
+        @pl.when(j + 1 < pairs)
+        def _():
+            edges_in(j + 1)
+
+        first_sweep(1, j)
 
     def both_next(j):
         for i in range(2):
             next_source(j, i)
 
-    def source_in(j):
-        source_arrived(j)
-        own_sweep(1, j)
-
-    over_pairs(own_sweep, 0)
-    over_pairs(first_sweep, 0)
+    def second_sweep(t):
+        def rest(c):
+            @pl.when(c < chunks - 2)
+            def _():
+                inner_product(c + 2, 0)
+
+        def body(c, _):
+            if t == 1:
+                rest(c)
+            finish(t, c)
+            if t == 0:
+                rest(c)
+            return 0
+
+        lax.fori_loop(0, chunks, body, 0)
+
+    def both_of(step, j):
+        step(j)
+
+        @pl.when(j == 0)
+        def _():
+            lax.fori_loop(0, 2, inner_product, 0)
+
+    over_pairs(both_of, opening)
     second_sweep(0)
     over_pairs(both_next)
-    over_pairs(source_in)
-    over_pairs(first_sweep, 1)
+    edges_in(0)
+    over_pairs(both_of, opening_again)
     second_sweep(1)
 
     for c in range(chunks):
@@ -403,11 +500,13 @@
 
     all_came(rsr, rs_ss.at[0])
     all_came(rsrp, rs_ss.at[1])
-    all_came(agr, ag_ss.at[0])
-    all_came(agrp, ag_ss.at[1])
+    all_came(agm, ag_ss.at[0])
+    all_came(age, ag_ss.at[1])
+    all_came(agrp, ag_ss.at[2])
 
     def all_left(d):
         all_came(hs.at[d], halo_ss.at[d])
+        all_came(e1.at[0, 0, pl.ds(0, 256), pl.ds(0, N)], nb_ss.at[d])
         all_came(p1s.at[d], p1_ss.at[d, 0])
         all_came(p1sp.at[d], p1_ss.at[d, 1])
 
@@ -428,6 +527,7 @@
     vmem = pl.BlockSpec(memory_space=pltpu.VMEM)
     smem = pl.BlockSpec(memory_space=pltpu.SMEM)
     anywhere = pl.BlockSpec(memory_space=pl.ANY)
+    hbm = pl.BlockSpec(memory_space=pltpu.HBM)
     dma = pltpu.SemaphoreType.DMA
 
     def body(*refs):
@@ -436,7 +536,7 @@
     return pl.pallas_call(
         body,
         out_shape=jax.ShapeDtypeStruct((rows // 8, columns), F32),
-        in_specs=[vmem, vmem, smem, smem, anywhere, anywhere],
+        in_specs=[vmem, vmem, smem, smem, hbm, hbm],
         out_specs=anywhere,
         scratch_shapes=[
             pltpu.VMEM((768, 2048), BF16),
@@ -444,7 +544,7 @@
             pltpu.VMEM((768, N), F32),
             pltpu.VMEM((1536, 1024), BF16),
             pltpu.VMEM((2, chunks // 2, 1024, PAIR), BF16),
-            pltpu.VMEM((2, 2, chunks // 2, H, PAIR), BF16),
+            pltpu.VMEM((2, 2 * (chunks // 2) - 1, H, PAIR), BF16),
             pltpu.VMEM((chunks, 2, 784, N), F32),
             pltpu.VMEM((chunks, 768, N), F32),
             pltpu.VMEM((chunks, 2, 2, H, N), F32),
@@ -458,9 +558,11 @@
             pltpu.VMEM((2, chunks, 1, N), F32),
             pltpu.VMEM((2, chunks, 7, 1, N), F32),
             pltpu.VMEM((chunks, 96, N), I16),
-            pltpu.VMEM((chunks, 7, 96, N), I16),
+            pltpu.VMEM((chunks, 7, 64, N), I16),
+            pltpu.VMEM((chunks, 7, 32, N), I16),
             pltpu.VMEM((chunks, 1, N), F32),
             pltpu.VMEM((chunks, 7, 1, N), F32),
+            pltpu.VMEM((2, 2, 16, N), BF16),
             pltpu.VMEM((96, chunks * N), F32),
             dma((2,)),
             dma((2,)),
@@ -469,8 +571,10 @@
             dma((2, chunks, 2, 2)),
             dma((2,)),
             dma((2, chunks, 2)),
+            dma((3,)),
+            dma((chunks, 3)),
             dma((2,)),
-            dma((chunks, 2)),
+            dma((2, 2)),
         ],
         compiler_params=pltpu.CompilerParams(
             collective_id=0, has_side_effects=True, vmem_limit_bytes=58 << 20

time: 63.6 us -> 64.9 us (1.020)
  Pallas kernels: 61.8 us -> 63.1 us
    pallas_call x1, Pallas kernels: 61.8 us -> 63.1 us  [shards(): pl.pallas_call(body, out_shape=jax.ShapeDtypeStruct((rows // 8, columns),...]
where the time goes in v3:
time: 64.9 us; the launch traced here: 64.7 us
  Pallas kernels  63.1 us (97%)
  local copies, waits for them, and re-layouts  1.62 us (2%)
    pallas_call x1, Pallas kernels, shards(): pl.pallas_call(body, out_shape=jax.ShapeDtypeStruct((rows // 8, columns),...  63.1 us
    unnamed x1, local copies, waits for them, and re-layouts  1.62 us

profile of v3, /device:TPU:0, one launch (start us, length us, event | category | flops | bytes accessed | tf_op | source)
XLA Modules:
  0.0 64.7 jit_solution(3499445547932877812)
XLA Ops:
  0.0 63.1 %shard_map.64 = f32[96,512]{1,0:T(8,128)} custom-call(s32[1,1024]{1,0:T(1,128)} %refs_0_.1, f32[768]{0:T(1024)} %refs_1_.1, f32[1,2]{1,0:T(1,128)} %refs_2_.1, f32[1,2]{1,0:T(1,128)} %refs_3_.1, f32[768,512]{1,0:T(8,128)} %refs_4_.1, bf16[1,768,2048]{2,1,0:T(8,128)(2,1)} %refs_5_.1), custom_call_target="tpu_custom_call" | custom-call | tf_op jit(solution)/shard_map/pallas_call | solution.py:536
  63.1 1.6 %copy.8 = f32[96,512]{1,0:T(8,128)} copy(f32[96,512]{1,0:T(8,128)} %shard_map.64) | data formatting | bytes 393216

commit v4 on v2

--- a/solution.py
+++ b/solution.py
@@ -11,7 +11,7 @@
 H = 128
 N = 128
 PAIR = 2 * N
-PEERS = ((2, 1), (1, 1), (3, 1), (2, 0), (0, 1), (1, 0), (3, 0))
+PEERS = ((2, 1), (0, 1), (2, 0), (1, 1), (3, 1), (1, 0), (3, 0))
 I16 = jnp.int16
 TOP = 32767.0
 
@@ -239,7 +239,8 @@
                     peak = peak_of(v)
                     p1sp[d, t, c, i : i + 1, :] = peak
                     p1s[d, t, c, i] = coded(v, peak)
-        start_both(edge_copy, t, c)
+            if b == 5:
+                start_both(edge_copy, t, c)
 
     def weighted(y):
         re = y[:768, 0:N] - y[768:, N : 2 * N]

time: 63.6 us -> 62.8 us (0.987)
  Pallas kernels: 61.8 us -> 61 us
    pallas_call x1, Pallas kernels: 61.8 us -> 61 us  [shards(): pl.pallas_call(body, out_shape=jax.ShapeDtypeStruct((rows // 8, columns),...]
where the time goes in v4:
time: 62.8 us; the launch traced here: 62.6 us
  Pallas kernels  61 us (97%)
  local copies, waits for them, and re-layouts  1.62 us (3%)
    pallas_call x1, Pallas kernels, shards(): pl.pallas_call(body, out_shape=jax.ShapeDtypeStruct((rows // 8, columns),...  61 us
    unnamed x1, local copies, waits for them, and re-layouts  1.62 us

profile of v4, /device:TPU:0, one launch (start us, length us, event | category | flops | bytes accessed | tf_op | source)
XLA Modules:
  0.0 62.6 jit_solution(12361242632374348608)
XLA Ops:
  0.0 61.0 %shard_map.64 = f32[96,512]{1,0:T(8,128)} custom-call(s32[1,1024]{1,0:T(1,128)} %refs_0_.1, f32[768]{0:T(1024)} %refs_1_.1, f32[1,2]{1,0:T(1,128)} %refs_2_.1, f32[1,2]{1,0:T(1,128)} %refs_3_.1, f32[768,512]{1,0:T(8,128)} %refs_4_.1, bf16[1,768,2048]{2,1,0:T(8,128)(2,1)} %refs_5_.1), custom_call_target="tpu_custom_call" | custom-call | tf_op jit(solution)/shard_map/pallas_call | solution.py:437
  61.0 1.6 %copy.8 = f32[96,512]{1,0:T(8,128)} copy(f32[96,512]{1,0:T(8,128)} %shard_map.64) | data formatting | bytes 393216
